TPU v7x, 32 devices: a whole 2x2x4 slice. The times are simulated.
32 devices in a mesh: gx: 8 (over y, x, core), gy: 4 (over z).
Axes of the slice: x: 2, y: 2, z: 4, core: 2. Of those that a mesh axis runs over, the one named last changes fastest.
Arguments:
- snapshots: bfloat16 [2, 1, 256, 256, 512], P(None, None, 'gx', 'gy'), may hold values from -12 to 12
- start: float32 [1, 32, 256, 256], P(None, None, 'gx', 'gy'), may hold values from -6 to 6
Outputs:
- basis_field: float32 [1, 32, 256, 256], P(None, None, 'gx', 'gy')
- phi: float32 [1, 2, 32, 32], replicated
All inputs are finite; a program needn't handle non-finite values.
Results may differ from a plain program's by a relative error of at most 0.0005.
Values may be sent and summed in bfloat16 or wider, within the bound.
A program may use at most 64 MiB of HBM per device.

v0:
```python
import jax
import jax.numpy as jnp
from jax import lax
from jax.sharding import PartitionSpec as P

ITERS = 4
precise = lax.Precision.HIGHEST


def swapped(x, axis, apart):
    return lax.ppermute(x, axis, [(i, i ^ 1 << apart) for i in range(lax.axis_size(axis))])


def passed_along(block, axis, distance):
    devices = range(lax.axis_size(axis))
    route = [(i - distance, i) for i in devices if i - distance in devices]
    return lax.ppermute(block, axis, route)


def inverse_factor(matrix):
    factor = jnp.linalg.cholesky(matrix)
    identity = jnp.broadcast_to(jnp.eye(matrix.shape[-1], dtype=matrix.dtype), matrix.shape)
    inverse = lax.linalg.triangular_solve(factor, identity, left_side=True, lower=True)
    return (factor, inverse)


def apply_inverse(inverse, right_side):
    return jnp.einsum("...kj,...jm->...km", inverse, right_side, precision=precise)


def shift_solve(inverse, right_matrix):
    inner = apply_inverse(inverse, right_matrix)
    return apply_inverse(jnp.swapaxes(inverse, -1, -2), inner)


def project(local_side):
    return lax.psum(local_side, ("gx", "gy"))


def gram_of(grown):
    return jnp.einsum("fkm,fjm->fkj", grown, grown, precision=precise)


def pair_grams(plus_terms, minus_terms):
    left_matrix = jnp.einsum("fkab,fjab->fkj", plus_terms, plus_terms, precision=precise)
    right_matrix = jnp.einsum("fkab,fjab->fkj", plus_terms, minus_terms, precision=precise)
    return (left_matrix, right_matrix)


def mirror_fields(stacked, rows, cols):
    moved = stacked
    for bit_number in range(lax.axis_size("gx").bit_length() - 1):
        moved = swapped(moved, "gx", bit_number)
    for bit_number in range(lax.axis_size("gy").bit_length() - 1):
        moved = swapped(moved, "gy", bit_number)
    lead = moved.shape[:-1]
    turned = moved.reshape(lead + (rows, cols))[..., ::-1, ::-1]
    return turned.reshape(moved.shape)


def shift_terms(field):
    rows = field.shape[2]
    cols = field.shape[3]
    below = passed_along(field[:, :, :1, :], "gx", -1)
    beside = passed_along(field[:, :, :, :1], "gy", -1)
    last_row_device = lax.axis_index("gx") == lax.axis_size("gx") - 1
    last_col_device = lax.axis_index("gy") == lax.axis_size("gy") - 1
    row_weight = jnp.where((jnp.arange(rows) == rows - 1) & last_row_device, 0.0, 1.0).astype(
        jnp.float32
    )
    col_weight = jnp.where((jnp.arange(cols) == cols - 1) & last_col_device, 0.0, 1.0).astype(
        jnp.float32
    )
    row_extended = jnp.concatenate([field, below], axis=2)
    col_extended = jnp.concatenate([field, beside], axis=3)
    row_plus = (row_extended[:, :, 1:] + row_extended[:, :, :-1]) * row_weight[:, None]
    row_minus = row_extended[:, :, 1:] - row_extended[:, :, :-1]
    col_plus = (col_extended[:, :, :, 1:] + col_extended[:, :, :, :-1]) * col_weight
    col_minus = col_extended[:, :, :, 1:] - col_extended[:, :, :, :-1]
    row_lhs, row_rhs = pair_grams(row_plus, row_minus)
    col_lhs, col_rhs = pair_grams(col_plus, col_minus)
    return (row_lhs, row_rhs, col_lhs, col_rhs)


def body(snapshots, start):
    frames, basis_count, rows, cols = start.shape
    upper_half = lax.axis_index("gx") < lax.axis_size("gx") // 2
    start_flat = start.reshape(frames, basis_count, rows * cols)
    own = snapshots.astype(jnp.float32).reshape(2, frames, rows * cols, -1)

    def local_side(weights, weights_mirror):
        p_real = jnp.einsum("fkm,fms->fks", weights, own[0], precision=precise)
        p_imag = jnp.einsum("fkm,fms->fks", weights, own[1], precision=precise)
        q_real = jnp.einsum("fkm,fms->fks", weights_mirror, own[0], precision=precise)
        q_imag = jnp.einsum("fkm,fms->fks", weights_mirror, own[1], precision=precise)
        first = jnp.where(upper_half, p_real - q_imag, p_imag + q_real)
        second = jnp.where(upper_half, -p_imag - q_real, p_real - q_imag)
        return jnp.concatenate([first, second], axis=-1)

    start_mirror = mirror_fields(start_flat[None], rows, cols)[0]
    basis = start_flat
    basis_mirror = start_mirror
    for step_index in range(ITERS):
        side = project(local_side(basis, basis_mirror))
        half = side.shape[-1] // 2
        side_first = side[..., :half]
        side_second = side[..., half:]
        g_real = jnp.einsum("fks,fms->fkm", side_first, own[0], precision=precise) - jnp.einsum(
            "fks,fms->fkm", side_second, own[1], precision=precise
        )
        g_imag = jnp.einsum("fks,fms->fkm", side_first, own[1], precision=precise) + jnp.einsum(
            "fks,fms->fkm", side_second, own[0], precision=precise
        )
        moved = mirror_fields(jnp.stack([g_real, g_imag]), rows, cols)
        grown = jnp.where(upper_half, g_real + moved[0], g_imag - moved[1])
        grown_mirror = jnp.where(upper_half, moved[1] - g_imag, moved[0] + g_real)
        grown, grown_mirror = (grown, grown_mirror)
        gram = lax.psum(gram_of(grown), ("gx", "gy"))
        factor, inverse = inverse_factor(gram)
        basis = apply_inverse(inverse, grown)
        basis_mirror = apply_inverse(inverse, grown_mirror)
    field = basis.reshape(frames, basis_count, rows, cols)
    local_terms = shift_terms(field)
    row_lhs, row_rhs, col_lhs, col_rhs = lax.psum(
        (local_terms[0], local_terms[1], local_terms[2], local_terms[3]), ("gx", "gy")
    )
    factors, inverses = inverse_factor(jnp.stack([row_lhs, col_lhs]))
    phi = jnp.swapaxes(shift_solve(inverses, jnp.stack([row_rhs, col_rhs])), 0, 1)
    return (field, phi)


def solution(mesh):
    return jax.shard_map(
        body,
        mesh=mesh,
        in_specs=(P(None, None, "gx", "gy", None), P(None, None, "gx", "gy")),
        out_specs=(P(None, None, "gx", "gy"), P()),
        check_vma=False,
    )
```

profile of v0, /device:TPU:0, one launch (start us, length us, event | category | flops | bytes accessed | tf_op | source)
XLA Modules:
  0.0 1151.4 jit_solution(10792632579092109949)
XLA Ops:
  14.2 5.4 collective-permute-done.1
  24.0 3.4 collective-permute-done.2
  30.0 4.3 collective-permute-done.3
  37.7 9.2 collective-permute-done.4
  53.8 125.0 %all-reduce.6.cloned.1.call-done = f32[1,32,1024]{2,1,0:T(8,128)} async-done(((f32[1,32,1024]{2,1,0:T(8,128)}), f32[1,32,1024]{2,1,0:T(8,128)}) %all-reduce.6.cloned.1.call-update) | async-done | bytes 131088 | tf_op jit(solution)/shard_map/psum | solution.py:37
  191.0 12.5 %collective-permute-done.6 = f32[2,1,32,2048]{3,2,1,0:T(8,128)S(1)} collective-permute-done((f32[2,1,32,2048]{3,2,1,0:T(8,128)S(1)}, f32[2,1,32,2048]{3,2,1,0:T(8,128)S(1)}, u32[]{:S(2)}, u32[]{:S(2)}) %collective-permute-start.6) | collective-permute-done | bytes 524320 | tf_op jit(solution)/shard_map/ppermute | solution.py:11
  204.9 11.6 %collective-permute-done.7 = f32[2,1,32,2048]{3,2,1,0:T(8,128)S(1)} collective-permute-done((f32[2,1,32,2048]{3,2,1,0:T(8,128)S(1)}, f32[2,1,32,2048]{3,2,1,0:T(8,128)S(1)}, u32[]{:S(2)}, u32[]{:S(2)}) %collective-permute-start.7) | collective-permute-done | bytes 524320 | tf_op jit(solution)/shard_map/ppermute | solution.py:11
  218.0 10.8 collective-permute-done.8
  230.3 22.1 %collective-permute-done.9 = f32[2,1,32,2048]{3,2,1,0:T(8,128)S(1)} collective-permute-done((f32[2,1,32,2048]{3,2,1,0:T(8,128)S(1)}, f32[2,1,32,2048]{3,2,1,0:T(8,128)S(1)}, u32[]{:S(2)}, u32[]{:S(2)}) %collective-permute-start.9) | collective-permute-done | bytes 524320 | tf_op jit(solution)/shard_map/ppermute | solution.py:11
  259.4 38.0 %psum.85 = f32[1,32,32]{1,2,0:T(8,128)S(1)} all-reduce(f32[1,32,32]{1,2,0:T(8,128)S(1)} %convolution_bitcast_fusion.10), channel_id=1, replica_groups=mesh['gx'=8,'gy'=4] {'gx','gy'}, use_global_device_ids=true, to_apply=%region_1.2 | all-reduce | flops 1024 | bytes 8192 | tf_op jit(solution)/shard_map/psum | solution.py:118
  310.2 125.8 %all-reduce.8.cloned.1.call-done = f32[1,32,1024]{2,1,0:T(8,128)} async-done(((f32[1,32,1024]{2,1,0:T(8,128)}), f32[1,32,1024]{2,1,0:T(8,128)}) %all-reduce.8.cloned.1.call-update) | async-done | bytes 131088 | tf_op jit(solution)/shard_map/psum | solution.py:37
  448.2 12.5 %collective-permute-done.11 = f32[2,1,32,2048]{3,2,1,0:T(8,128)S(1)} collective-permute-done((f32[2,1,32,2048]{3,2,1,0:T(8,128)S(1)}, f32[2,1,32,2048]{3,2,1,0:T(8,128)S(1)}, u32[]{:S(2)}, u32[]{:S(2)}) %collective-permute-start.11) | collective-permute-done | bytes 524320 | tf_op jit(solution)/shard_map/ppermute | solution.py:11
  462.1 11.6 %collective-permute-done.12 = f32[2,1,32,2048]{3,2,1,0:T(8,128)S(1)} collective-permute-done((f32[2,1,32,2048]{3,2,1,0:T(8,128)S(1)}, f32[2,1,32,2048]{3,2,1,0:T(8,128)S(1)}, u32[]{:S(2)}, u32[]{:S(2)}) %collective-permute-start.12) | collective-permute-done | bytes 524320 | tf_op jit(solution)/shard_map/ppermute | solution.py:11
  475.3 10.8 collective-permute-done.13
  487.5 22.1 %collective-permute-done.14 = f32[2,1,32,2048]{3,2,1,0:T(8,128)S(1)} collective-permute-done((f32[2,1,32,2048]{3,2,1,0:T(8,128)S(1)}, f32[2,1,32,2048]{3,2,1,0:T(8,128)S(1)}, u32[]{:S(2)}, u32[]{:S(2)}) %collective-permute-start.14) | collective-permute-done | bytes 524320 | tf_op jit(solution)/shard_map/ppermute | solution.py:11
  516.6 38.1 %psum.87 = f32[1,32,32]{1,2,0:T(8,128)S(1)} all-reduce(f32[1,32,32]{1,2,0:T(8,128)S(1)} %convolution_bitcast_fusion.9), channel_id=1, replica_groups=mesh['gx'=8,'gy'=4] {'gx','gy'}, use_global_device_ids=true, to_apply=%region_5.8 | all-reduce | flops 1024 | bytes 8192 | tf_op jit(solution)/shard_map/psum | solution.py:118
  567.5 125.8 %all-reduce.10.cloned.1.call-done = f32[1,32,1024]{2,1,0:T(8,128)} async-done(((f32[1,32,1024]{2,1,0:T(8,128)}), f32[1,32,1024]{2,1,0:T(8,128)}) %all-reduce.10.cloned.1.call-update) | async-done | bytes 131088 | tf_op jit(solution)/shard_map/psum | solution.py:37
  705.4 12.5 %collective-permute-done.16 = f32[2,1,32,2048]{3,2,1,0:T(8,128)S(1)} collective-permute-done((f32[2,1,32,2048]{3,2,1,0:T(8,128)S(1)}, f32[2,1,32,2048]{3,2,1,0:T(8,128)S(1)}, u32[]{:S(2)}, u32[]{:S(2)}) %collective-permute-start.16) | collective-permute-done | bytes 524320 | tf_op jit(solution)/shard_map/ppermute | solution.py:11
  719.4 11.6 %collective-permute-done.17 = f32[2,1,32,2048]{3,2,1,0:T(8,128)S(1)} collective-permute-done((f32[2,1,32,2048]{3,2,1,0:T(8,128)S(1)}, f32[2,1,32,2048]{3,2,1,0:T(8,128)S(1)}, u32[]{:S(2)}, u32[]{:S(2)}) %collective-permute-start.17) | collective-permute-done | bytes 524320 | tf_op jit(solution)/shard_map/ppermute | solution.py:11
  732.5 10.8 collective-permute-done.18
  744.7 22.1 %collective-permute-done.19 = f32[2,1,32,2048]{3,2,1,0:T(8,128)S(1)} collective-permute-done((f32[2,1,32,2048]{3,2,1,0:T(8,128)S(1)}, f32[2,1,32,2048]{3,2,1,0:T(8,128)S(1)}, u32[]{:S(2)}, u32[]{:S(2)}) %collective-permute-start.19) | collective-permute-done | bytes 524320 | tf_op jit(solution)/shard_map/ppermute | solution.py:11
  773.8 38.2 %psum.89 = f32[1,32,32]{1,2,0:T(8,128)S(1)} all-reduce(f32[1,32,32]{1,2,0:T(8,128)S(1)} %convolution_bitcast_fusion.8), channel_id=1, replica_groups=mesh['gx'=8,'gy'=4] {'gx','gy'}, use_global_device_ids=true, to_apply=%region_7.10 | all-reduce | flops 1024 | bytes 8192 | tf_op jit(solution)/shard_map/psum | solution.py:118
  824.9 125.8 %all-reduce.12.cloned.1.call-done = f32[1,32,1024]{2,1,0:T(8,128)} async-done(((f32[1,32,1024]{2,1,0:T(8,128)}), f32[1,32,1024]{2,1,0:T(8,128)}) %all-reduce.12.cloned.1.call-update) | async-done | bytes 131088 | tf_op jit(solution)/shard_map/psum | solution.py:37
  962.8 12.5 %collective-permute-done.21 = f32[2,1,32,2048]{3,2,1,0:T(8,128)S(1)} collective-permute-done((f32[2,1,32,2048]{3,2,1,0:T(8,128)S(1)}, f32[2,1,32,2048]{3,2,1,0:T(8,128)S(1)}, u32[]{:S(2)}, u32[]{:S(2)}) %collective-permute-start.21) | collective-permute-done | bytes 524320 | tf_op jit(solution)/shard_map/ppermute | solution.py:11
  976.8 11.6 %collective-permute-done.22 = f32[2,1,32,2048]{3,2,1,0:T(8,128)S(1)} collective-permute-done((f32[2,1,32,2048]{3,2,1,0:T(8,128)S(1)}, f32[2,1,32,2048]{3,2,1,0:T(8,128)S(1)}, u32[]{:S(2)}, u32[]{:S(2)}) %collective-permute-start.22) | collective-permute-done | bytes 524320 | tf_op jit(solution)/shard_map/ppermute | solution.py:11
  989.9 10.8 collective-permute-done.23
  1002.2 22.0 %collective-permute-done.24 = f32[2,1,32,2048]{3,2,1,0:T(8,128)S(1)} collective-permute-done((f32[2,1,32,2048]{3,2,1,0:T(8,128)S(1)}, f32[2,1,32,2048]{3,2,1,0:T(8,128)S(1)}, u32[]{:S(2)}, u32[]{:S(2)}) %collective-permute-start.24) | collective-permute-done | bytes 524320 | tf_op jit(solution)/shard_map/ppermute | solution.py:11
  1026.1 38.0 %psum.91 = f32[1,32,32]{1,2,0:T(8,128)S(1)} all-reduce(f32[1,32,32]{1,2,0:T(8,128)S(1)} %convolution_bitcast_fusion.7), channel_id=1, replica_groups=mesh['gx'=8,'gy'=4] {'gx','gy'}, use_global_device_ids=true, to_apply=%region_9.12 | all-reduce | flops 1024 | bytes 8192 | tf_op jit(solution)/shard_map/psum | solution.py:118
  1075.8 12.2 %collective-permute-done.26 = f32[1,32,32,1]{3,1,2,0:T(8,128)S(1)} collective-permute-done((f32[1,32,32,1]{3,1,2,0:T(8,128)S(1)}, f32[1,32,32,1]{3,1,2,0:T(8,128)S(1)}, u32[]{:S(2)}, u32[]{:S(2)}) %collective-permute-start.26) | collective-permute-done | bytes 4128 | tf_op jit(solution)/shard_map/ppermute | solution.py:17
  1091.3 40.9 %all-reduce = (f32[1,1,32,32]{2,3,1,0:T(8,128)S(1)}, f32[1,1,32,32]{2,3,1,0:T(8,128)S(1)}, f32[1,1,32,32]{3,2,1,0:T(8,128)S(1)}, f32[1,1,32,32]{3,2,1,0:T(8,128)S(1)}) all-reduce(f32[1,1,32,32]{2,3,1,0:T(8,128)S(1)} %convolution_bitcast_fusion.5, ...), channel_id=1, replica_groups=mesh['gx'=8,'gy'=4] {'gx','gy'}, use_global_device_ids=true, to_apply=%region_10.13 | all-reduce | flops 4096 | bytes 32768 | tf_op jit(solution)/shard_map/psum | solution.py:124
  1132.4 5.9 custom-call.13
  1138.5 4.9 custom-call.14
  (207 shorter events, 167.9 us)
Async XLA Ops:
  7.2 171.7 %all-reduce.6.cloned.1.call-start = ((), (), s32[]{:S(2)}) async-start(), calls=%async_computation | async-start | bytes 262144 | tf_op jit(solution)/shard_map/psum | solution.py:37
  8.4 1.7 collective-permute-start
  10.2 9.5 collective-permute-start.1
  19.6 7.8 collective-permute-start.2
  24.0 13.7 %copy-start = (bf16[1,1,32,64,512]{4,3,2,1,0:T(8,128)(2,1)}, bf16[1,1,32,64,512]{4,3,2,1,0:T(8,128)(2,1)S(1)}, u32[]{:S(2)}) copy-start(bf16[1,1,32,64,512]{4,3,2,1,0:T(8,128)(2,1)S(1)} %get-tuple-element.15) | copy-start | bytes 6291460
  27.4 6.9 collective-permute-start.3
  34.3 12.6 %collective-permute-start.4 = (f32[1,1,32,2048]{3,2,1,0:T(8,128)S(1)}, f32[1,1,32,2048]{3,2,1,0:T(8,128)S(1)}, u32[]{:S(2)}, u32[]{:S(2)}) collective-permute-start(f32[1,1,32,2048]{3,2,1,0:T(8,128)S(1)} %collective-permute-done.3), channel_id=1, source_target_pairs={{0,2},{1,3},{2,0},{3,1},{4,6},{5,7},{6,4},{7,5},{8,10},{9,11},{10,... | collective-permute-start | bytes 786440 | tf_op jit(solution)/shard_map/ppermute | solution.py:11
  53.8 382.3 %all-reduce.8.cloned.1.call-start = ((), (), s32[]{:S(2)}) async-start(), calls=%async_computation.1 | async-start | bytes 262144 | tf_op jit(solution)/shard_map/psum | solution.py:37
  187.5 2.0 collective-permute-start.5
  189.5 14.0 %collective-permute-start.6 = (f32[2,1,32,2048]{3,2,1,0:T(8,128)S(1)}, f32[2,1,32,2048]{3,2,1,0:T(8,128)S(1)}, u32[]{:S(2)}, u32[]{:S(2)}) collective-permute-start(f32[2,1,32,2048]{3,2,1,0:T(8,128)S(1)} %collective-permute-done.5), channel_id=1, source_target_pairs={{0,8},{4,12},{8,0},{12,4},{16,24},{20,28},{24,16},{28,20},{1,9},{5... | collective-permute-start | bytes 1572872 | tf_op jit(solution)/shard_map/ppermute | solution.py:11
  203.5 13.1 %collective-permute-start.7 = (f32[2,1,32,2048]{3,2,1,0:T(8,128)S(1)}, f32[2,1,32,2048]{3,2,1,0:T(8,128)S(1)}, u32[]{:S(2)}, u32[]{:S(2)}) collective-permute-start(f32[2,1,32,2048]{3,2,1,0:T(8,128)S(1)} %collective-permute-done.6), channel_id=1, source_target_pairs={{0,16},{4,20},{8,24},{12,28},{16,0},{20,4},{24,8},{28,12},{1,17},{... | collective-permute-start | bytes 1572872 | tf_op jit(solution)/shard_map/ppermute | solution.py:11
  216.6 12.3 %collective-permute-start.8 = (f32[2,1,32,2048]{3,2,1,0:T(8,128)S(1)}, f32[2,1,32,2048]{3,2,1,0:T(8,128)S(1)}, u32[]{:S(2)}, u32[]{:S(2)}) collective-permute-start(f32[2,1,32,2048]{3,2,1,0:T(8,128)S(1)} %collective-permute-done.7), channel_id=1, source_target_pairs={{0,1},{1,0},{2,3},{3,2},{4,5},{5,4},{6,7},{7,6},{8,9},{9,8},{10,11... | collective-permute-start | bytes 1572872 | tf_op jit(solution)/shard_map/ppermute | solution.py:11
  228.8 23.5 %collective-permute-start.9 = (f32[2,1,32,2048]{3,2,1,0:T(8,128)S(1)}, f32[2,1,32,2048]{3,2,1,0:T(8,128)S(1)}, u32[]{:S(2)}, u32[]{:S(2)}) collective-permute-start(f32[2,1,32,2048]{3,2,1,0:T(8,128)S(1)} %collective-permute-done.8), channel_id=1, source_target_pairs={{0,2},{1,3},{2,0},{3,1},{4,6},{5,7},{6,4},{7,5},{8,10},{9,11},{10,... | collective-permute-start | bytes 1572872 | tf_op jit(solution)/shard_map/ppermute | solution.py:11
  310.2 383.1 %all-reduce.10.cloned.1.call-start = ((), (), s32[]{:S(2)}) async-start(), calls=%async_computation.2 | async-start | bytes 262144 | tf_op jit(solution)/shard_map/psum | solution.py:37
  444.7 2.0 collective-permute-start.10
  446.7 14.0 %collective-permute-start.11 = (f32[2,1,32,2048]{3,2,1,0:T(8,128)S(1)}, f32[2,1,32,2048]{3,2,1,0:T(8,128)S(1)}, u32[]{:S(2)}, u32[]{:S(2)}) collective-permute-start(f32[2,1,32,2048]{3,2,1,0:T(8,128)S(1)} %collective-permute-done.10), channel_id=1, source_target_pairs={{0,8},{4,12},{8,0},{12,4},{16,24},{20,28},{24,16},{28,20},{1,9},{5... | collective-permute-start | bytes 1572872 | tf_op jit(solution)/shard_map/ppermute | solution.py:11
  460.7 13.1 %collective-permute-start.12 = (f32[2,1,32,2048]{3,2,1,0:T(8,128)S(1)}, f32[2,1,32,2048]{3,2,1,0:T(8,128)S(1)}, u32[]{:S(2)}, u32[]{:S(2)}) collective-permute-start(f32[2,1,32,2048]{3,2,1,0:T(8,128)S(1)} %collective-permute-done.11), channel_id=1, source_target_pairs={{0,16},{4,20},{8,24},{12,28},{16,0},{20,4},{24,8},{28,12},{1,17},{... | collective-permute-start | bytes 1572872 | tf_op jit(solution)/shard_map/ppermute | solution.py:11
  473.8 12.3 %collective-permute-start.13 = (f32[2,1,32,2048]{3,2,1,0:T(8,128)S(1)}, f32[2,1,32,2048]{3,2,1,0:T(8,128)S(1)}, u32[]{:S(2)}, u32[]{:S(2)}) collective-permute-start(f32[2,1,32,2048]{3,2,1,0:T(8,128)S(1)} %collective-permute-done.12), channel_id=1, source_target_pairs={{0,1},{1,0},{2,3},{3,2},{4,5},{5,4},{6,7},{7,6},{8,9},{9,8},{10,11... | collective-permute-start | bytes 1572872 | tf_op jit(solution)/shard_map/ppermute | solution.py:11
  486.0 23.5 %collective-permute-start.14 = (f32[2,1,32,2048]{3,2,1,0:T(8,128)S(1)}, f32[2,1,32,2048]{3,2,1,0:T(8,128)S(1)}, u32[]{:S(2)}, u32[]{:S(2)}) collective-permute-start(f32[2,1,32,2048]{3,2,1,0:T(8,128)S(1)} %collective-permute-done.13), channel_id=1, source_target_pairs={{0,2},{1,3},{2,0},{3,1},{4,6},{5,7},{6,4},{7,5},{8,10},{9,11},{10,... | collective-permute-start | bytes 1572872 | tf_op jit(solution)/shard_map/ppermute | solution.py:11
  567.5 383.3 %all-reduce.12.cloned.1.call-start = ((), (), s32[]{:S(2)}) async-start(), calls=%async_computation.3 | async-start | bytes 262144 | tf_op jit(solution)/shard_map/psum | solution.py:37
  702.0 2.0 collective-permute-start.15
  703.9 14.0 %collective-permute-start.16 = (f32[2,1,32,2048]{3,2,1,0:T(8,128)S(1)}, f32[2,1,32,2048]{3,2,1,0:T(8,128)S(1)}, u32[]{:S(2)}, u32[]{:S(2)}) collective-permute-start(f32[2,1,32,2048]{3,2,1,0:T(8,128)S(1)} %collective-permute-done.15), channel_id=1, source_target_pairs={{0,8},{4,12},{8,0},{12,4},{16,24},{20,28},{24,16},{28,20},{1,9},{5... | collective-permute-start | bytes 1572872 | tf_op jit(solution)/shard_map/ppermute | solution.py:11
  717.9 13.1 %collective-permute-start.17 = (f32[2,1,32,2048]{3,2,1,0:T(8,128)S(1)}, f32[2,1,32,2048]{3,2,1,0:T(8,128)S(1)}, u32[]{:S(2)}, u32[]{:S(2)}) collective-permute-start(f32[2,1,32,2048]{3,2,1,0:T(8,128)S(1)} %collective-permute-done.16), channel_id=1, source_target_pairs={{0,16},{4,20},{8,24},{12,28},{16,0},{20,4},{24,8},{28,12},{1,17},{... | collective-permute-start | bytes 1572872 | tf_op jit(solution)/shard_map/ppermute | solution.py:11
  731.0 12.3 %collective-permute-start.18 = (f32[2,1,32,2048]{3,2,1,0:T(8,128)S(1)}, f32[2,1,32,2048]{3,2,1,0:T(8,128)S(1)}, u32[]{:S(2)}, u32[]{:S(2)}) collective-permute-start(f32[2,1,32,2048]{3,2,1,0:T(8,128)S(1)} %collective-permute-done.17), channel_id=1, source_target_pairs={{0,1},{1,0},{2,3},{3,2},{4,5},{5,4},{6,7},{7,6},{8,9},{9,8},{10,11... | collective-permute-start | bytes 1572872 | tf_op jit(solution)/shard_map/ppermute | solution.py:11
  743.3 23.5 %collective-permute-start.19 = (f32[2,1,32,2048]{3,2,1,0:T(8,128)S(1)}, f32[2,1,32,2048]{3,2,1,0:T(8,128)S(1)}, u32[]{:S(2)}, u32[]{:S(2)}) collective-permute-start(f32[2,1,32,2048]{3,2,1,0:T(8,128)S(1)} %collective-permute-done.18), channel_id=1, source_target_pairs={{0,2},{1,3},{2,0},{3,1},{4,6},{5,7},{6,4},{7,5},{8,10},{9,11},{10,... | collective-permute-start | bytes 1572872 | tf_op jit(solution)/shard_map/ppermute | solution.py:11
  959.4 2.0 collective-permute-start.20
  961.4 14.0 %collective-permute-start.21 = (f32[2,1,32,2048]{3,2,1,0:T(8,128)S(1)}, f32[2,1,32,2048]{3,2,1,0:T(8,128)S(1)}, u32[]{:S(2)}, u32[]{:S(2)}) collective-permute-start(f32[2,1,32,2048]{3,2,1,0:T(8,128)S(1)} %collective-permute-done.20), channel_id=1, source_target_pairs={{0,8},{4,12},{8,0},{12,4},{16,24},{20,28},{24,16},{28,20},{1,9},{5... | collective-permute-start | bytes 1572872 | tf_op jit(solution)/shard_map/ppermute | solution.py:11
  975.3 13.1 %collective-permute-start.22 = (f32[2,1,32,2048]{3,2,1,0:T(8,128)S(1)}, f32[2,1,32,2048]{3,2,1,0:T(8,128)S(1)}, u32[]{:S(2)}, u32[]{:S(2)}) collective-permute-start(f32[2,1,32,2048]{3,2,1,0:T(8,128)S(1)} %collective-permute-done.21), channel_id=1, source_target_pairs={{0,16},{4,20},{8,24},{12,28},{16,0},{20,4},{24,8},{28,12},{1,17},{... | collective-permute-start | bytes 1572872 | tf_op jit(solution)/shard_map/ppermute | solution.py:11
  988.4 12.3 %collective-permute-start.23 = (f32[2,1,32,2048]{3,2,1,0:T(8,128)S(1)}, f32[2,1,32,2048]{3,2,1,0:T(8,128)S(1)}, u32[]{:S(2)}, u32[]{:S(2)}) collective-permute-start(f32[2,1,32,2048]{3,2,1,0:T(8,128)S(1)} %collective-permute-done.22), channel_id=1, source_target_pairs={{0,1},{1,0},{2,3},{3,2},{4,5},{5,4},{6,7},{7,6},{8,9},{9,8},{10,11... | collective-permute-start | bytes 1572872 | tf_op jit(solution)/shard_map/ppermute | solution.py:11
  1000.7 23.5 %collective-permute-start.24 = (f32[2,1,32,2048]{3,2,1,0:T(8,128)S(1)}, f32[2,1,32,2048]{3,2,1,0:T(8,128)S(1)}, u32[]{:S(2)}, u32[]{:S(2)}) collective-permute-start(f32[2,1,32,2048]{3,2,1,0:T(8,128)S(1)} %collective-permute-done.23), channel_id=1, source_target_pairs={{0,2},{1,3},{2,0},{3,1},{4,6},{5,7},{6,4},{7,5},{8,10},{9,11},{10,... | collective-permute-start | bytes 1572872 | tf_op jit(solution)/shard_map/ppermute | solution.py:11
  1072.0 15.9 %collective-permute-start.26 = (f32[1,32,32,1]{3,1,2,0:T(8,128)S(1)}, f32[1,32,32,1]{3,1,2,0:T(8,128)S(1)}, u32[]{:S(2)}, u32[]{:S(2)}) collective-permute-start(f32[1,32,32,1]{3,1,2,0:T(8,128)S(1)} %bitcast.338), channel_id=1, source_target_pairs={{1,0},{2,1},{3,2},{5,4},{6,5},{7,6},{9,8},{10,9},{11,10},{13,12},{... | collective-permute-start | bytes 12296 | tf_op jit(solution)/shard_map/ppermute | solution.py:17
  1074.5 15.5 %collective-permute-start.25 = (f32[1,32,1,64]{3,1,2,0:T(8,128)S(1)}, f32[1,32,1,64]{3,1,2,0:T(8,128)S(1)}, u32[]{:S(2)}, u32[]{:S(2)}) collective-permute-start(f32[1,32,1,64]{3,1,2,0:T(8,128)S(1)} %slice.232), channel_id=1, source_target_pairs={{4,0},{8,4},{12,8},{16,12},{20,16},{24,20},{28,24},{5,1},{9,5},{13... | collective-permute-start | bytes 24584 | tf_op jit(solution)/shard_map/ppermute | solution.py:17
  (11 other events, 28.7 us)
Sparse Core Ops, SparseCore 0:
  53.9 124.9 all-reduce.5
  310.3 125.6 all-reduce.7
  567.6 125.6 all-reduce.9
  825.0 125.6 all-reduce.11
where the time goes:
time: 1160 us; the launch traced here: 1150 us
  waiting for transfers between devices  774 us (67%)
  blocking collectives  193 us (17%)
  matrix products  65.3 us (6%)
  other arithmetic  40.8 us (4%)
  starting transfers between devices  35.6 us (3%)
  local copies, waits for them, and re-layouts  28.2 us (2%)
  between operations  14.8 us (1%)
    psum x4, waiting for transfers between devices, project(): return lax.psum(local_side, ('gx', 'gy'))  502 us
    ppermute x25, waiting for transfers between devices, swapped(): lax.ppermute(x, axis, [(i, i ^ 1 << apart) for i in range(lax.axis_size(a...  259 us
    psum x4, blocking collectives, body(): gram = lax.psum(gram_of(grown), ('gx', 'gy'))  152 us
    psum x1, blocking collectives, body(): lax.psum((local_terms[0], local_terms[1], local_terms[2], local_terms[3])...  40.9 us
    ppermute x25, starting transfers between devices, swapped(): lax.ppermute(x, axis, [(i, i ^ 1 << apart) for i in range(lax.axis_size(a...  32.9 us
  transfers between devices with their start and end apart: 31, of which 30 were waited for; matrix products, arithmetic and copies ran while one was open for 1% of the time, Pallas kernels for 0%

commit v1 on v0

--- a/solution.py
+++ b/solution.py
@@ -34,7 +34,7 @@
 
 
 def project(local_side):
-    return lax.psum(local_side, ("gx", "gy"))
+    return jnp.sum(lax.all_gather(local_side, ("gx", "gy")), axis=0)
 
 
 def gram_of(grown):

time: 1160 us -> 920 us (0.79)
  waiting for transfers between devices: 774 us -> 523 us
    psum x4 -> x0, waiting for transfers between devices: 502 us -> none  [project(): return lax.psum(local_side, ('gx', 'gy'))]
    all_gather x0 -> x4, waiting for transfers between devices: none -> 252 us  [project(): return jnp.sum(lax.all_gather(local_side, ('gx', 'gy')), axis=0)]
where the time goes in v1:
time: 920 us; the launch traced here: 911 us
  waiting for transfers between devices  523 us (57%)
  blocking collectives  192 us (21%)
  matrix products  61.3 us (7%)
  other arithmetic  50.6 us (6%)
  starting transfers between devices  36.1 us (4%)
  local copies, waits for them, and re-layouts  33.6 us (4%)
  between operations  14.7 us (2%)
    ppermute x25, waiting for transfers between devices, swapped(): lax.ppermute(x, axis, [(i, i ^ 1 << apart) for i in range(lax.axis_size(a...  260 us
    all_gather x4, waiting for transfers between devices, project(): return jnp.sum(lax.all_gather(local_side, ('gx', 'gy')), axis=0)  252 us
    psum x4, blocking collectives, body(): gram = lax.psum(gram_of(grown), ('gx', 'gy'))  151 us
    psum x1, blocking collectives, body(): lax.psum((local_terms[0], local_terms[1], local_terms[2], local_terms[3])...  40.9 us
    ppermute x25, starting transfers between devices, swapped(): lax.ppermute(x, axis, [(i, i ^ 1 << apart) for i in range(lax.axis_size(a...  33.3 us
    another operation x16, other arithmetic, inverse_factor(): factor = jnp.linalg.cholesky(matrix)  20.4 us
    slice x20, local copies, waits for them, and re-layouts, body(): grown = jnp.where(upper_half, g_real + moved[0], g_imag - moved[1])  18.6 us
  transfers between devices with their start and end apart: 31, of which 30 were waited for; matrix products, arithmetic and copies ran while one was open for 1% of the time, Pallas kernels for 0%

profile of v1, /device:TPU:0, one launch (start us, length us, event | category | flops | bytes accessed | tf_op | source)
XLA Modules:
  0.0 911.5 jit_solution(4932431353959962915)
XLA Ops:
  14.2 5.4 collective-permute-done.1
  24.0 3.4 collective-permute-done.2
  30.0 4.3 collective-permute-done.3
  37.7 9.2 %collective-permute-done.4 = f32[1,1,32,2048]{3,2,1,0:T(8,128)S(1)} collective-permute-done((f32[1,1,32,2048]{3,2,1,0:T(8,128)S(1)}, f32[1,1,32,2048]{3,2,1,0:T(8,128)S(1)}, u32[]{:S(2)}, u32[]{:S(2)}) %collective-permute-start.4) | collective-permute-done | bytes 262176 | tf_op jit(solution)/shard_map/ppermute | solution.py:11
  53.8 62.3 %all-gather.9.cloned.1.call-done = f32[32,32,1024]{2,1,0:T(8,128)} async-done(((f32[1,32,1024]{2,1,0:T(8,128)}), f32[32,32,1024]{2,1,0:T(8,128)}) %all-gather.9.cloned.1.call-update) | async-done | bytes 4194320 | tf_op jit(solution)/shard_map/all_gather | solution.py:37
  129.4 12.8 %collective-permute-done.6 = f32[2,1,32,2048]{3,2,1,0:T(8,128)S(1)} collective-permute-done((f32[2,1,32,2048]{3,2,1,0:T(8,128)S(1)}, f32[2,1,32,2048]{3,2,1,0:T(8,128)S(1)}, u32[]{:S(2)}, u32[]{:S(2)}) %collective-permute-start.6) | collective-permute-done | bytes 524320 | tf_op jit(solution)/shard_map/ppermute | solution.py:11
  143.7 11.7 %collective-permute-done.7 = f32[2,1,32,2048]{3,2,1,0:T(8,128)S(1)} collective-permute-done((f32[2,1,32,2048]{3,2,1,0:T(8,128)S(1)}, f32[2,1,32,2048]{3,2,1,0:T(8,128)S(1)}, u32[]{:S(2)}, u32[]{:S(2)}) %collective-permute-start.7) | collective-permute-done | bytes 524320 | tf_op jit(solution)/shard_map/ppermute | solution.py:11
  156.9 10.9 %collective-permute-done.8 = f32[2,1,32,2048]{3,2,1,0:T(8,128)S(1)} collective-permute-done((f32[2,1,32,2048]{3,2,1,0:T(8,128)S(1)}, f32[2,1,32,2048]{3,2,1,0:T(8,128)S(1)}, u32[]{:S(2)}, u32[]{:S(2)}) %collective-permute-start.8) | collective-permute-done | bytes 524320 | tf_op jit(solution)/shard_map/ppermute | solution.py:11
  169.5 22.0 %collective-permute-done.9 = f32[2,1,32,2048]{3,2,1,0:T(8,128)S(1)} collective-permute-done((f32[2,1,32,2048]{3,2,1,0:T(8,128)S(1)}, f32[2,1,32,2048]{3,2,1,0:T(8,128)S(1)}, u32[]{:S(2)}, u32[]{:S(2)}) %collective-permute-start.9) | collective-permute-done | bytes 524320 | tf_op jit(solution)/shard_map/ppermute | solution.py:11
  200.3 37.7 %psum.56 = f32[1,32,32]{1,2,0:T(8,128)S(1)} all-reduce(f32[1,32,32]{1,2,0:T(8,128)S(1)} %convolution_bitcast_fusion.10), channel_id=1, replica_groups=mesh['gx'=8,'gy'=4] {'gx','gy'}, use_global_device_ids=true, to_apply=%region_1.2 | all-reduce | flops 1024 | bytes 8192 | tf_op jit(solution)/shard_map/psum | solution.py:118
  250.8 63.1 %all-gather.11.cloned.1.call-done = f32[32,32,1024]{2,1,0:T(8,128)} async-done(((f32[1,32,1024]{2,1,0:T(8,128)}), f32[32,32,1024]{2,1,0:T(8,128)}) %all-gather.11.cloned.1.call-update) | async-done | bytes 4194320 | tf_op jit(solution)/shard_map/all_gather | solution.py:37
  327.3 12.8 %collective-permute-done.11 = f32[2,1,32,2048]{3,2,1,0:T(8,128)S(1)} collective-permute-done((f32[2,1,32,2048]{3,2,1,0:T(8,128)S(1)}, f32[2,1,32,2048]{3,2,1,0:T(8,128)S(1)}, u32[]{:S(2)}, u32[]{:S(2)}) %collective-permute-start.11) | collective-permute-done | bytes 524320 | tf_op jit(solution)/shard_map/ppermute | solution.py:11
  341.6 11.7 %collective-permute-done.12 = f32[2,1,32,2048]{3,2,1,0:T(8,128)S(1)} collective-permute-done((f32[2,1,32,2048]{3,2,1,0:T(8,128)S(1)}, f32[2,1,32,2048]{3,2,1,0:T(8,128)S(1)}, u32[]{:S(2)}, u32[]{:S(2)}) %collective-permute-start.12) | collective-permute-done | bytes 524320 | tf_op jit(solution)/shard_map/ppermute | solution.py:11
  354.7 10.9 %collective-permute-done.13 = f32[2,1,32,2048]{3,2,1,0:T(8,128)S(1)} collective-permute-done((f32[2,1,32,2048]{3,2,1,0:T(8,128)S(1)}, f32[2,1,32,2048]{3,2,1,0:T(8,128)S(1)}, u32[]{:S(2)}, u32[]{:S(2)}) %collective-permute-start.13) | collective-permute-done | bytes 524320 | tf_op jit(solution)/shard_map/ppermute | solution.py:11
  367.3 22.0 %collective-permute-done.14 = f32[2,1,32,2048]{3,2,1,0:T(8,128)S(1)} collective-permute-done((f32[2,1,32,2048]{3,2,1,0:T(8,128)S(1)}, f32[2,1,32,2048]{3,2,1,0:T(8,128)S(1)}, u32[]{:S(2)}, u32[]{:S(2)}) %collective-permute-start.14) | collective-permute-done | bytes 524320 | tf_op jit(solution)/shard_map/ppermute | solution.py:11
  398.1 37.7 %psum.57 = f32[1,32,32]{1,2,0:T(8,128)S(1)} all-reduce(f32[1,32,32]{1,2,0:T(8,128)S(1)} %convolution_bitcast_fusion.9), channel_id=1, replica_groups=mesh['gx'=8,'gy'=4] {'gx','gy'}, use_global_device_ids=true, to_apply=%region_5.8 | all-reduce | flops 1024 | bytes 8192 | tf_op jit(solution)/shard_map/psum | solution.py:118
  448.7 63.1 %all-gather.13.cloned.1.call-done = f32[32,32,1024]{2,1,0:T(8,128)} async-done(((f32[1,32,1024]{2,1,0:T(8,128)}), f32[32,32,1024]{2,1,0:T(8,128)}) %all-gather.13.cloned.1.call-update) | async-done | bytes 4194320 | tf_op jit(solution)/shard_map/all_gather | solution.py:37
  525.1 12.8 %collective-permute-done.16 = f32[2,1,32,2048]{3,2,1,0:T(8,128)S(1)} collective-permute-done((f32[2,1,32,2048]{3,2,1,0:T(8,128)S(1)}, f32[2,1,32,2048]{3,2,1,0:T(8,128)S(1)}, u32[]{:S(2)}, u32[]{:S(2)}) %collective-permute-start.16) | collective-permute-done | bytes 524320 | tf_op jit(solution)/shard_map/ppermute | solution.py:11
  539.4 11.7 %collective-permute-done.17 = f32[2,1,32,2048]{3,2,1,0:T(8,128)S(1)} collective-permute-done((f32[2,1,32,2048]{3,2,1,0:T(8,128)S(1)}, f32[2,1,32,2048]{3,2,1,0:T(8,128)S(1)}, u32[]{:S(2)}, u32[]{:S(2)}) %collective-permute-start.17) | collective-permute-done | bytes 524320 | tf_op jit(solution)/shard_map/ppermute | solution.py:11
  552.6 10.9 %collective-permute-done.18 = f32[2,1,32,2048]{3,2,1,0:T(8,128)S(1)} collective-permute-done((f32[2,1,32,2048]{3,2,1,0:T(8,128)S(1)}, f32[2,1,32,2048]{3,2,1,0:T(8,128)S(1)}, u32[]{:S(2)}, u32[]{:S(2)}) %collective-permute-start.18) | collective-permute-done | bytes 524320 | tf_op jit(solution)/shard_map/ppermute | solution.py:11
  565.1 22.0 %collective-permute-done.19 = f32[2,1,32,2048]{3,2,1,0:T(8,128)S(1)} collective-permute-done((f32[2,1,32,2048]{3,2,1,0:T(8,128)S(1)}, f32[2,1,32,2048]{3,2,1,0:T(8,128)S(1)}, u32[]{:S(2)}, u32[]{:S(2)}) %collective-permute-start.19) | collective-permute-done | bytes 524320 | tf_op jit(solution)/shard_map/ppermute | solution.py:11
  596.0 37.9 %psum.58 = f32[1,32,32]{1,2,0:T(8,128)S(1)} all-reduce(f32[1,32,32]{1,2,0:T(8,128)S(1)} %convolution_bitcast_fusion.8), channel_id=1, replica_groups=mesh['gx'=8,'gy'=4] {'gx','gy'}, use_global_device_ids=true, to_apply=%region_7.10 | all-reduce | flops 1024 | bytes 8192 | tf_op jit(solution)/shard_map/psum | solution.py:118
  646.7 63.1 %all-gather.15.cloned.1.call-done = f32[32,32,1024]{2,1,0:T(8,128)} async-done(((f32[1,32,1024]{2,1,0:T(8,128)}), f32[32,32,1024]{2,1,0:T(8,128)}) %all-gather.15.cloned.1.call-update) | async-done | bytes 4194320 | tf_op jit(solution)/shard_map/all_gather | solution.py:37
  723.1 12.8 %collective-permute-done.21 = f32[2,1,32,2048]{3,2,1,0:T(8,128)S(1)} collective-permute-done((f32[2,1,32,2048]{3,2,1,0:T(8,128)S(1)}, f32[2,1,32,2048]{3,2,1,0:T(8,128)S(1)}, u32[]{:S(2)}, u32[]{:S(2)}) %collective-permute-start.21) | collective-permute-done | bytes 524320 | tf_op jit(solution)/shard_map/ppermute | solution.py:11
  737.4 11.7 %collective-permute-done.22 = f32[2,1,32,2048]{3,2,1,0:T(8,128)S(1)} collective-permute-done((f32[2,1,32,2048]{3,2,1,0:T(8,128)S(1)}, f32[2,1,32,2048]{3,2,1,0:T(8,128)S(1)}, u32[]{:S(2)}, u32[]{:S(2)}) %collective-permute-start.22) | collective-permute-done | bytes 524320 | tf_op jit(solution)/shard_map/ppermute | solution.py:11
  750.6 10.9 %collective-permute-done.23 = f32[2,1,32,2048]{3,2,1,0:T(8,128)S(1)} collective-permute-done((f32[2,1,32,2048]{3,2,1,0:T(8,128)S(1)}, f32[2,1,32,2048]{3,2,1,0:T(8,128)S(1)}, u32[]{:S(2)}, u32[]{:S(2)}) %collective-permute-start.23) | collective-permute-done | bytes 524320 | tf_op jit(solution)/shard_map/ppermute | solution.py:11
  763.2 22.0 %collective-permute-done.24 = f32[2,1,32,2048]{3,2,1,0:T(8,128)S(1)} collective-permute-done((f32[2,1,32,2048]{3,2,1,0:T(8,128)S(1)}, f32[2,1,32,2048]{3,2,1,0:T(8,128)S(1)}, u32[]{:S(2)}, u32[]{:S(2)}) %collective-permute-start.24) | collective-permute-done | bytes 524320 | tf_op jit(solution)/shard_map/ppermute | solution.py:11
  787.1 37.7 %psum.59 = f32[1,32,32]{1,2,0:T(8,128)S(1)} all-reduce(f32[1,32,32]{1,2,0:T(8,128)S(1)} %convolution_bitcast_fusion.7), channel_id=1, replica_groups=mesh['gx'=8,'gy'=4] {'gx','gy'}, use_global_device_ids=true, to_apply=%region_9.12 | all-reduce | flops 1024 | bytes 8192 | tf_op jit(solution)/shard_map/psum | solution.py:118
  836.4 11.6 %collective-permute-done.26 = f32[1,32,32,1]{3,1,2,0:T(8,128)S(1)} collective-permute-done((f32[1,32,32,1]{3,1,2,0:T(8,128)S(1)}, f32[1,32,32,1]{3,1,2,0:T(8,128)S(1)}, u32[]{:S(2)}, u32[]{:S(2)}) %collective-permute-start.26) | collective-permute-done | bytes 4128 | tf_op jit(solution)/shard_map/ppermute | solution.py:17
  851.4 40.9 %all-reduce = (f32[1,1,32,32]{2,3,1,0:T(8,128)S(1)}, f32[1,1,32,32]{2,3,1,0:T(8,128)S(1)}, f32[1,1,32,32]{3,2,1,0:T(8,128)S(1)}, f32[1,1,32,32]{3,2,1,0:T(8,128)S(1)}) all-reduce(f32[1,1,32,32]{2,3,1,0:T(8,128)S(1)} %convolution_bitcast_fusion.5, ...), channel_id=1, replica_groups=mesh['gx'=8,'gy'=4] {'gx','gy'}, use_global_device_ids=true, to_apply=%region_10.13 | all-reduce | flops 4096 | bytes 32768 | tf_op jit(solution)/shard_map/psum | solution.py:124
  892.5 5.9 custom-call.13
  898.6 4.9 custom-call.14
  (203 shorter events, 178.6 us)
Async XLA Ops:
  7.2 108.9 %all-gather.9.cloned.1.call-start = ((), (), s32[]{:S(2)}) async-start(), calls=%async_computation | async-start | bytes 4325376 | tf_op jit(solution)/shard_map/all_gather | solution.py:37
  8.4 1.7 collective-permute-start
  10.2 9.5 %collective-permute-start.1 = (f32[1,1,32,2048]{3,2,1,0:T(8,128)S(1)}, f32[1,1,32,2048]{3,2,1,0:T(8,128)S(1)}, u32[]{:S(2)}, u32[]{:S(2)}) collective-permute-start(f32[1,1,32,2048]{3,2,1,0:T(8,128)S(1)} %collective-permute-done), channel_id=1, source_target_pairs={{0,8},{4,12},{8,0},{12,4},{16,24},{20,28},{24,16},{28,20},{1,9},{5... | collective-permute-start | bytes 786440 | tf_op jit(solution)/shard_map/ppermute | solution.py:11
  19.6 7.8 collective-permute-start.2
  24.0 13.7 %copy-start = (bf16[1,1,32,64,512]{4,3,2,1,0:T(8,128)(2,1)}, bf16[1,1,32,64,512]{4,3,2,1,0:T(8,128)(2,1)S(1)}, u32[]{:S(2)}) copy-start(bf16[1,1,32,64,512]{4,3,2,1,0:T(8,128)(2,1)S(1)} %get-tuple-element.17) | copy-start | bytes 6291460
  27.4 6.9 collective-permute-start.3
  34.3 12.6 %collective-permute-start.4 = (f32[1,1,32,2048]{3,2,1,0:T(8,128)S(1)}, f32[1,1,32,2048]{3,2,1,0:T(8,128)S(1)}, u32[]{:S(2)}, u32[]{:S(2)}) collective-permute-start(f32[1,1,32,2048]{3,2,1,0:T(8,128)S(1)} %collective-permute-done.3), channel_id=1, source_target_pairs={{0,2},{1,3},{2,0},{3,1},{4,6},{5,7},{6,4},{7,5},{8,10},{9,11},{10,... | collective-permute-start | bytes 786440 | tf_op jit(solution)/shard_map/ppermute | solution.py:11
  53.8 260.2 %all-gather.11.cloned.1.call-start = ((), (), s32[]{:S(2)}) async-start(), calls=%async_computation.1 | async-start | bytes 4325376 | tf_op jit(solution)/shard_map/all_gather | solution.py:37
  126.2 2.0 collective-permute-start.5
  128.2 14.1 %collective-permute-start.6 = (f32[2,1,32,2048]{3,2,1,0:T(8,128)S(1)}, f32[2,1,32,2048]{3,2,1,0:T(8,128)S(1)}, u32[]{:S(2)}, u32[]{:S(2)}) collective-permute-start(f32[2,1,32,2048]{3,2,1,0:T(8,128)S(1)} %collective-permute-done.5), channel_id=1, source_target_pairs={{0,8},{4,12},{8,0},{12,4},{16,24},{20,28},{24,16},{28,20},{1,9},{5... | collective-permute-start | bytes 1572872 | tf_op jit(solution)/shard_map/ppermute | solution.py:11
  142.3 13.2 %collective-permute-start.7 = (f32[2,1,32,2048]{3,2,1,0:T(8,128)S(1)}, f32[2,1,32,2048]{3,2,1,0:T(8,128)S(1)}, u32[]{:S(2)}, u32[]{:S(2)}) collective-permute-start(f32[2,1,32,2048]{3,2,1,0:T(8,128)S(1)} %collective-permute-done.6), channel_id=1, source_target_pairs={{0,16},{4,20},{8,24},{12,28},{16,0},{20,4},{24,8},{28,12},{1,17},{... | collective-permute-start | bytes 1572872 | tf_op jit(solution)/shard_map/ppermute | solution.py:11
  155.5 12.4 %collective-permute-start.8 = (f32[2,1,32,2048]{3,2,1,0:T(8,128)S(1)}, f32[2,1,32,2048]{3,2,1,0:T(8,128)S(1)}, u32[]{:S(2)}, u32[]{:S(2)}) collective-permute-start(f32[2,1,32,2048]{3,2,1,0:T(8,128)S(1)} %collective-permute-done.7), channel_id=1, source_target_pairs={{0,1},{1,0},{2,3},{3,2},{4,5},{5,4},{6,7},{7,6},{8,9},{9,8},{10,11... | collective-permute-start | bytes 1572872 | tf_op jit(solution)/shard_map/ppermute | solution.py:11
  167.8 23.6 %collective-permute-start.9 = (f32[2,1,32,2048]{3,2,1,0:T(8,128)S(1)}, f32[2,1,32,2048]{3,2,1,0:T(8,128)S(1)}, u32[]{:S(2)}, u32[]{:S(2)}) collective-permute-start(f32[2,1,32,2048]{3,2,1,0:T(8,128)S(1)} %collective-permute-done.8), channel_id=1, source_target_pairs={{0,2},{1,3},{2,0},{3,1},{4,6},{5,7},{6,4},{7,5},{8,10},{9,11},{10,... | collective-permute-start | bytes 1572872 | tf_op jit(solution)/shard_map/ppermute | solution.py:11
  250.8 261.0 %all-gather.13.cloned.1.call-start = ((), (), s32[]{:S(2)}) async-start(), calls=%async_computation.2 | async-start | bytes 4325376 | tf_op jit(solution)/shard_map/all_gather | solution.py:37
  324.0 2.0 collective-permute-start.10
  326.0 14.1 %collective-permute-start.11 = (f32[2,1,32,2048]{3,2,1,0:T(8,128)S(1)}, f32[2,1,32,2048]{3,2,1,0:T(8,128)S(1)}, u32[]{:S(2)}, u32[]{:S(2)}) collective-permute-start(f32[2,1,32,2048]{3,2,1,0:T(8,128)S(1)} %collective-permute-done.10), channel_id=1, source_target_pairs={{0,8},{4,12},{8,0},{12,4},{16,24},{20,28},{24,16},{28,20},{1,9},{5... | collective-permute-start | bytes 1572872 | tf_op jit(solution)/shard_map/ppermute | solution.py:11
  340.1 13.2 %collective-permute-start.12 = (f32[2,1,32,2048]{3,2,1,0:T(8,128)S(1)}, f32[2,1,32,2048]{3,2,1,0:T(8,128)S(1)}, u32[]{:S(2)}, u32[]{:S(2)}) collective-permute-start(f32[2,1,32,2048]{3,2,1,0:T(8,128)S(1)} %collective-permute-done.11), channel_id=1, source_target_pairs={{0,16},{4,20},{8,24},{12,28},{16,0},{20,4},{24,8},{28,12},{1,17},{... | collective-permute-start | bytes 1572872 | tf_op jit(solution)/shard_map/ppermute | solution.py:11
  353.3 12.4 %collective-permute-start.13 = (f32[2,1,32,2048]{3,2,1,0:T(8,128)S(1)}, f32[2,1,32,2048]{3,2,1,0:T(8,128)S(1)}, u32[]{:S(2)}, u32[]{:S(2)}) collective-permute-start(f32[2,1,32,2048]{3,2,1,0:T(8,128)S(1)} %collective-permute-done.12), channel_id=1, source_target_pairs={{0,1},{1,0},{2,3},{3,2},{4,5},{5,4},{6,7},{7,6},{8,9},{9,8},{10,11... | collective-permute-start | bytes 1572872 | tf_op jit(solution)/shard_map/ppermute | solution.py:11
  365.7 23.6 %collective-permute-start.14 = (f32[2,1,32,2048]{3,2,1,0:T(8,128)S(1)}, f32[2,1,32,2048]{3,2,1,0:T(8,128)S(1)}, u32[]{:S(2)}, u32[]{:S(2)}) collective-permute-start(f32[2,1,32,2048]{3,2,1,0:T(8,128)S(1)} %collective-permute-done.13), channel_id=1, source_target_pairs={{0,2},{1,3},{2,0},{3,1},{4,6},{5,7},{6,4},{7,5},{8,10},{9,11},{10,... | collective-permute-start | bytes 1572872 | tf_op jit(solution)/shard_map/ppermute | solution.py:11
  448.7 261.1 %all-gather.15.cloned.1.call-start = ((), (), s32[]{:S(2)}) async-start(), calls=%async_computation.3 | async-start | bytes 4325376 | tf_op jit(solution)/shard_map/all_gather | solution.py:37
  521.9 2.0 collective-permute-start.15
  523.8 14.1 %collective-permute-start.16 = (f32[2,1,32,2048]{3,2,1,0:T(8,128)S(1)}, f32[2,1,32,2048]{3,2,1,0:T(8,128)S(1)}, u32[]{:S(2)}, u32[]{:S(2)}) collective-permute-start(f32[2,1,32,2048]{3,2,1,0:T(8,128)S(1)} %collective-permute-done.15), channel_id=1, source_target_pairs={{0,8},{4,12},{8,0},{12,4},{16,24},{20,28},{24,16},{28,20},{1,9},{5... | collective-permute-start | bytes 1572872 | tf_op jit(solution)/shard_map/ppermute | solution.py:11
  537.9 13.2 %collective-permute-start.17 = (f32[2,1,32,2048]{3,2,1,0:T(8,128)S(1)}, f32[2,1,32,2048]{3,2,1,0:T(8,128)S(1)}, u32[]{:S(2)}, u32[]{:S(2)}) collective-permute-start(f32[2,1,32,2048]{3,2,1,0:T(8,128)S(1)} %collective-permute-done.16), channel_id=1, source_target_pairs={{0,16},{4,20},{8,24},{12,28},{16,0},{20,4},{24,8},{28,12},{1,17},{... | collective-permute-start | bytes 1572872 | tf_op jit(solution)/shard_map/ppermute | solution.py:11
  551.1 12.4 %collective-permute-start.18 = (f32[2,1,32,2048]{3,2,1,0:T(8,128)S(1)}, f32[2,1,32,2048]{3,2,1,0:T(8,128)S(1)}, u32[]{:S(2)}, u32[]{:S(2)}) collective-permute-start(f32[2,1,32,2048]{3,2,1,0:T(8,128)S(1)} %collective-permute-done.17), channel_id=1, source_target_pairs={{0,1},{1,0},{2,3},{3,2},{4,5},{5,4},{6,7},{7,6},{8,9},{9,8},{10,11... | collective-permute-start | bytes 1572872 | tf_op jit(solution)/shard_map/ppermute | solution.py:11
  563.5 23.6 %collective-permute-start.19 = (f32[2,1,32,2048]{3,2,1,0:T(8,128)S(1)}, f32[2,1,32,2048]{3,2,1,0:T(8,128)S(1)}, u32[]{:S(2)}, u32[]{:S(2)}) collective-permute-start(f32[2,1,32,2048]{3,2,1,0:T(8,128)S(1)} %collective-permute-done.18), channel_id=1, source_target_pairs={{0,2},{1,3},{2,0},{3,1},{4,6},{5,7},{6,4},{7,5},{8,10},{9,11},{10,... | collective-permute-start | bytes 1572872 | tf_op jit(solution)/shard_map/ppermute | solution.py:11
  719.9 2.0 collective-permute-start.20
  721.9 14.1 %collective-permute-start.21 = (f32[2,1,32,2048]{3,2,1,0:T(8,128)S(1)}, f32[2,1,32,2048]{3,2,1,0:T(8,128)S(1)}, u32[]{:S(2)}, u32[]{:S(2)}) collective-permute-start(f32[2,1,32,2048]{3,2,1,0:T(8,128)S(1)} %collective-permute-done.20), channel_id=1, source_target_pairs={{0,8},{4,12},{8,0},{12,4},{16,24},{20,28},{24,16},{28,20},{1,9},{5... | collective-permute-start | bytes 1572872 | tf_op jit(solution)/shard_map/ppermute | solution.py:11
  736.0 13.2 %collective-permute-start.22 = (f32[2,1,32,2048]{3,2,1,0:T(8,128)S(1)}, f32[2,1,32,2048]{3,2,1,0:T(8,128)S(1)}, u32[]{:S(2)}, u32[]{:S(2)}) collective-permute-start(f32[2,1,32,2048]{3,2,1,0:T(8,128)S(1)} %collective-permute-done.21), channel_id=1, source_target_pairs={{0,16},{4,20},{8,24},{12,28},{16,0},{20,4},{24,8},{28,12},{1,17},{... | collective-permute-start | bytes 1572872 | tf_op jit(solution)/shard_map/ppermute | solution.py:11
  749.2 12.4 %collective-permute-start.23 = (f32[2,1,32,2048]{3,2,1,0:T(8,128)S(1)}, f32[2,1,32,2048]{3,2,1,0:T(8,128)S(1)}, u32[]{:S(2)}, u32[]{:S(2)}) collective-permute-start(f32[2,1,32,2048]{3,2,1,0:T(8,128)S(1)} %collective-permute-done.22), channel_id=1, source_target_pairs={{0,1},{1,0},{2,3},{3,2},{4,5},{5,4},{6,7},{7,6},{8,9},{9,8},{10,11... | collective-permute-start | bytes 1572872 | tf_op jit(solution)/shard_map/ppermute | solution.py:11
  761.5 23.6 %collective-permute-start.24 = (f32[2,1,32,2048]{3,2,1,0:T(8,128)S(1)}, f32[2,1,32,2048]{3,2,1,0:T(8,128)S(1)}, u32[]{:S(2)}, u32[]{:S(2)}) collective-permute-start(f32[2,1,32,2048]{3,2,1,0:T(8,128)S(1)} %collective-permute-done.23), channel_id=1, source_target_pairs={{0,2},{1,3},{2,0},{3,1},{4,6},{5,7},{6,4},{7,5},{8,10},{9,11},{10,... | collective-permute-start | bytes 1572872 | tf_op jit(solution)/shard_map/ppermute | solution.py:11
  832.7 15.3 %collective-permute-start.26 = (f32[1,32,32,1]{3,1,2,0:T(8,128)S(1)}, f32[1,32,32,1]{3,1,2,0:T(8,128)S(1)}, u32[]{:S(2)}, u32[]{:S(2)}) collective-permute-start(f32[1,32,32,1]{3,1,2,0:T(8,128)S(1)} %bitcast.342), channel_id=1, source_target_pairs={{1,0},{2,1},{3,2},{5,4},{6,5},{7,6},{9,8},{10,9},{11,10},{13,12},{... | collective-permute-start | bytes 12296 | tf_op jit(solution)/shard_map/ppermute | solution.py:17
  835.1 14.9 %collective-permute-start.25 = (f32[1,32,1,64]{3,1,2,0:T(8,128)S(1)}, f32[1,32,1,64]{3,1,2,0:T(8,128)S(1)}, u32[]{:S(2)}, u32[]{:S(2)}) collective-permute-start(f32[1,32,1,64]{3,1,2,0:T(8,128)S(1)} %slice.232), channel_id=1, source_target_pairs={{4,0},{8,4},{12,8},{16,12},{20,16},{24,20},{28,24},{5,1},{9,5},{13... | collective-permute-start | bytes 24584 | tf_op jit(solution)/shard_map/ppermute | solution.py:17
  (7 other events, 13.1 us)
Sparse Core Ops, SparseCore 0:
  53.9 62.1 all-gather.8
  250.9 62.9 all-gather.10
  448.8 62.9 all-gather.12
  646.8 62.9 all-gather.14
